TPU v7x, 32 devices: a whole 2x2x4 slice. The times are simulated.
32 devices in a mesh: pole: 4 (over y, core), dom: 8 (over z, x).
Axes of the slice: x: 2, y: 2, z: 4, core: 2. Of those that a mesh axis runs over, the one named last changes fastest.
Arguments:
- initial_block: bfloat16 [8, 8, 512, 256], P('dom'), may hold values from -24 to 24
- coupling: bfloat16 [8, 8, 512, 512], P('dom'), may hold values from -0.125 to 0.125
- pivots: bfloat16 [4, 8, 8, 2, 512, 512], P('pole', 'dom'), may hold values from -0.125 to 0.125
- interface: bfloat16 [4, 8, 3, 2, 512, 512], P('pole', 'dom'), may hold values from -0.1875 to 0.1875
- pole_values: float32 [4, 4], P('pole'), may hold values from 0.5 to 1.5
Outputs:
- filtered_basis: float32 [8, 8, 512, 256], P('dom', 'pole')
- rayleigh: float32 [256, 256], replicated
All inputs are finite; a program needn't handle non-finite values.
Results may differ from a plain program's by a relative error of at most 0.008.
Values sent between devices are 32-bit elements; how exact they have to be, the bound alone decides.
No kernel may reach another device: no remote copies, remote signals or barrier semaphores. Data moves between devices by JAX's collectives and lax.ppermute only.
A program may use at most 192 MiB of HBM per device.

v0:
```python
import jax
import jax.numpy as jnp
from jax import lax
from jax.sharding import PartitionSpec as P

B = 512
M = 256


def shifted(x, axis, by):
    length = lax.axis_size(axis)
    pairs = [(i, i + by) for i in range(length) if 0 <= i + by < length]
    return lax.ppermute(x, axis, pairs)


def lower_solve(factor, right_side):
    return lax.linalg.triangular_solve(factor, right_side, left_side=True, lower=True)


def complex_product(matrix, vectors):
    block_order = matrix.shape[1]
    half_width = vectors.shape[1] // 2
    stacked = matrix.reshape(2 * block_order, block_order)
    stacked_out = jnp.dot(stacked, vectors.astype(jnp.bfloat16), preferred_element_type=jnp.float32)
    real_part = stacked_out[:block_order, :half_width] - stacked_out[block_order:, half_width:]
    imag_part = stacked_out[:block_order, half_width:] + stacked_out[block_order:, :half_width]
    return jnp.concatenate([real_part, imag_part], axis=1)


def real_product(matrix, vectors):
    return jnp.dot(matrix, vectors.astype(jnp.bfloat16), preferred_element_type=jnp.float32)


def transposed_product(matrix, vectors):
    return lax.dot_general(
        matrix,
        vectors.astype(jnp.bfloat16),
        (((0,), (0,)), ((), ())),
        preferred_element_type=jnp.float32,
    )


def inner_products(left, right_side):
    return lax.dot_general(
        left,
        right_side,
        (((0,), (0,)), ((), ())),
        precision=lax.Precision.HIGHEST,
        preferred_element_type=jnp.float32,
    )


def partition_solve(inverse, coupled, source):
    previous = jnp.roll(coupled, 1, axis=0)
    initial = jnp.zeros(source.shape[1:], jnp.float32)

    def forward_step(carried, members):
        block_inverse, given, couple_prev = members
        result = complex_product(block_inverse, given + transposed_product(couple_prev, carried))
        return (result, result)

    unused, forward = lax.scan(forward_step, initial, (inverse, source, previous))

    def backward_step(carried, members):
        block_inverse, partial_value, couple_next = members
        result = partial_value + complex_product(block_inverse, real_product(couple_next, carried))
        return (result, result)

    unused, backward = lax.scan(backward_step, initial, (inverse, forward, coupled), reverse=True)
    return backward


def on_device(initial_block, coupling, pivots, interface, pole_values):
    blocks = coupling.shape[1]
    coupled = coupling[0]
    inverse = pivots[0, 0]
    factors = interface[0, 0]
    real_start = initial_block[0].astype(jnp.float32)
    source = jnp.concatenate([real_start, jnp.zeros_like(real_start)], axis=-1)
    first = partition_solve(inverse, coupled, source)
    bottom = first[blocks - 1]
    top = first[0]
    top_next = shifted(top, "dom", -1)
    below = complex_product(factors[0], bottom) - complex_product(factors[1], top_next)
    topmost = lax.axis_index("dom") == lax.axis_size("dom") - 1
    above = jnp.where(
        topmost, jnp.zeros_like(top_next), top_next - complex_product(factors[2], below)
    )
    link = coupled[blocks - 1]
    lifted = transposed_product(link, below)
    arriving = shifted(lifted, "dom", 1)
    update = source.at[0].add(arriving)
    update = update.at[blocks - 1].add(real_product(link, above))
    second = partition_solve(inverse, coupled, update)
    real_z = pole_values[0, 0]
    imag_z = pole_values[0, 1]
    real_w = pole_values[0, 2]
    imag_w = pole_values[0, 3]
    real_x = second[..., :M]
    imag_x = second[..., M:]
    filtered_term = real_w * real_x - imag_w * imag_x
    shifted_term = (
        (real_w * real_z - imag_w * imag_z) * real_x
        - (real_w * imag_z + imag_w * real_z) * imag_x
        - real_w * real_start
    )
    count = blocks // lax.axis_size("pole")
    summed = lax.psum(filtered_term, "pole")
    offset = lax.axis_index("pole") * count
    own_rows = lax.dynamic_slice_in_dim(summed, offset, count, 0).reshape(count * B, M)
    gram_part = inner_products(own_rows, own_rows)
    projected_part = inner_products(
        summed.reshape(blocks * B, M), shifted_term.reshape(blocks * B, M)
    )
    gram_total, projected_total = lax.psum((gram_part, projected_part), ("pole", "dom"))
    row_total = blocks * B * lax.axis_size("dom")
    gram = gram_total / row_total
    projected = projected_total / row_total
    factor = jnp.linalg.cholesky(gram)
    filtered_basis = lower_solve(factor, own_rows.T).T.reshape(1, count, B, M)
    middle = lower_solve(factor, projected)
    rayleigh = lower_solve(factor, middle.T).T
    return (filtered_basis, rayleigh)


def solution(mesh):
    in_specs = (
        P("dom", None, None, None),
        P("dom", None, None, None),
        P("pole", "dom", None, None, None, None),
        P("pole", "dom", None, None, None, None),
        P("pole", None),
    )
    out_specs = (P("dom", "pole", None, None), P())
    return jax.shard_map(
        on_device, mesh=mesh, in_specs=in_specs, out_specs=out_specs, check_vma=False
    )
```

profile of v0, /device:TPU:0, one launch (start us, length us, event | category | flops | bytes accessed | tf_op | source)
XLA Modules:
  0.0 687.2 jit_solution(11109018124211285651)
XLA Ops:
  7.2 4.2 slice_bitcast_fusion
  12.5 2.9 copy.17
  18.0 4.2 concatenate.76
  24.6 4.3 broadcast.158.clone.2
  29.7 65.2 %while.65 = (s32[]{:T(128)}, bf16[512,512]{0,1:T(8,128)(2,1)}, f32[8,512,512]{1,2,0:T(8,128)}, bf16[8,2,512,512]{3,2,1,0:T(8,128)(2,1)}, f32[8,512,512]{1,2,0:T(8,128)}, /*index=5*/bf16[8,512,512]{2,1,0:T(8,128)(2,1)}, s32[]{:T(128)}) while((s32[]{:T(128)}, bf16[512,512]{0,1:T(8,128)(2,1)}, f32[8,512,512]{1,2,0:T(8,128)}, ...), condition=%wide.region_1.2_spmd, body=%wide.region_0.1_spmd.sunk | while | flops 806617088 | bytes 17302612 | solution.py:62
  95.0 4.3 broadcast.158.clone.1
  99.3 67.7 %while.68 = (s32[]{:T(128)}, bf16[512,512]{0,1:T(8,128)(2,1)}, f32[8,512,512]{1,2,0:T(8,128)}, f32[8,512,512]{1,2,0:T(8,128)}, bf16[8,2,512,512]{3,2,1,0:T(8,128...) while((s32[]{:T(128)}, bf16[512,512]{0,1:T(8,128)(2,1)}, ...), condition=%wide.region_3.4_spmd.clone, body=%wide.region_2.3_spmd.clone.sunk | while | flops 807403520 | bytes 15204483 | solution.py:69
  173.8 22.5 %collective-permute-done = f32[512,512]{0,1:T(8,128)S(1)} collective-permute-done((f32[512,512]{0,1:T(8,128)S(1)}, f32[512,512]{0,1:T(8,128)S(1)}, u32[]{:S(2)}, u32[]{:S(2)}) %collective-permute-start) | collective-permute-done | bytes 1048608 | tf_op jit(solution)/shard_map/ppermute | solution.py:13
  200.0 6.1 collective-permute-start.1
  207.7 18.7 %collective-permute-done.1 = f32[512,512]{0,1:T(8,128)} collective-permute-done((f32[512,512]{0,1:T(8,128)}, f32[512,512]{0,1:T(8,128)}, u32[]{:S(2)}, u32[]{:S(2)}) %collective-permute-start.1) | collective-permute-done | bytes 1048608 | tf_op jit(solution)/shard_map/ppermute | solution.py:13
  228.8 2.9 fusion.66
  231.7 4.3 broadcast.158.clone
  236.8 65.4 %while.66 = (s32[]{:T(128)}, bf16[512,512]{0,1:T(8,128)(2,1)}, f32[8,512,512]{1,2,0:T(8,128)}, bf16[8,2,512,512]{3,2,1,0:T(8,128)(2,1)}, f32[8,512,512]{1,2,0:T(8,128)}, /*index=5*/bf16[8,512,512]{2,1,0:T(8,128)(2,1)}, s32[]{:T(128)}) while((s32[]{:T(128)}, bf16[512,512]{0,1:T(8,128)(2,1)}, f32[8,512,512]{1,2,0:T(8,128)}, ...), condition=%wide.region_5.6_spmd, body=%wide.region_4.5_spmd.sunk | while | flops 806617088 | bytes 17302612 | solution.py:62
  302.3 4.3 broadcast.158
  306.6 67.7 %while.69 = (s32[]{:T(128)}, bf16[512,512]{0,1:T(8,128)(2,1)}, f32[8,512,512]{1,2,0:T(8,128)}, f32[8,512,512]{1,2,0:T(8,128)}, bf16[8,2,512,512]{3,2,1,0:T(8,128...) while((s32[]{:T(128)}, bf16[512,512]{0,1:T(8,128)(2,1)}, ...), condition=%wide.region_7.8_spmd.clone, body=%wide.region_6.7_spmd.clone.sunk | while | flops 807403520 | bytes 15204483 | solution.py:69
  374.3 7.7 %multiply_subtract_fusion = f32[8,512,256]{1,2,0:T(8,128)} fusion(f32[8,512,512]{1,2,0:T(8,128)} %get-tuple-element.338, f32[]{:T(128)} %bitcast.27, f32[]{:T(128)} %bitcast.8), kind=kLoop, calls=%fused_computation.67 | loop fusion | flops 3145728 | bytes 12582920 | tf_op jit(solution)/shard_map/sub | solution.py:101
  387.1 81.9 %all-reduce.6.cloned.1.call-done = f32[8,512,256]{1,2,0:T(8,128)} async-done(((f32[8,512,256]{1,2,0:T(8,128)}), f32[8,512,256]{1,2,0:T(8,128)}) %all-reduce.6.cloned.1.call-update) | async-done | bytes 4194320 | tf_op jit(solution)/shard_map/psum | solution.py:108
  472.1 9.1 %fusion.61 = f32[256,256]{0,1:T(8,128)} fusion(f32[8,512,256]{1,2,0:T(8,128)S(1)} %copy-done.5, f32[8,512,512]{1,2,0:T(8,128)} %get-tuple-element.338, f32[]{:T(128)S(6)} %add.171, f32[]{:T(128)S(6)} %sub.71, f32[]{:T(128)} %bitcast.8, bf16[1,8,512,256]{2,3,1,0:T(8,128)(2,1)S(1)} %copy-done.3), kind=kOutput, calls=%fused_computation.82 | convolution fusion | flops 3227516928 | bytes 14942220 | tf_op jit(solution)/shard_map/dot_general | solution.py:44
  481.6 129.2 %all-reduce.8.cloned.1.call-done = (f32[256,256]{0,1:T(8,128)}, f32[256,256]{0,1:T(8,128)}) async-done(((f32[256,256]{0,1:T(8,128)}, f32[256,256]{0,1:T(8,128)}), (f32[256,256]{0,1:T(8,128)}, f32[256,256]{0,1:T(8,128)})) %all-reduce.8.cloned.1.call-update) | async-done | bytes 524304 | tf_op jit(solution)/shard_map/psum | solution.py:115
  613.1 11.7 %cholesky.50 = f32[128,128]{1,0:T(8,128)S(1)} custom-call(f32[128,128]{1,0:T(8,128)S(1)} %cholesky.118), custom_call_target="Cholesky" | custom-call | tf_op jit(solution)/shard_map/jit(cholesky)/cholesky | solution.py:119
  624.8 10.0 %custom-call.17 = f32[1,128,128]{1,2,0:T(8,128)S(1)} custom-call(f32[1,128,128]{2,1,0:T(8,128)S(1)} %get-tuple-element.517), custom_call_target="InvertDiagBlocksLowerTriangular" | custom-call | tf_op jit(solution)/shard_map/jit(cholesky)/cholesky | solution.py:119
  635.3 11.7 %cholesky.105 = f32[128,128]{1,0:T(8,128)S(1)} custom-call(f32[128,128]{1,0:T(8,128)S(1)} %convolution_subtract_fusion.3), custom_call_target="Cholesky" | custom-call | tf_op jit(solution)/shard_map/jit(cholesky)/cholesky | solution.py:119
  649.8 4.0 while.67
  653.7 19.7 %custom-call.18 = f32[2,128,128]{1,2,0:T(8,128)S(1)} custom-call(f32[2,128,128]{2,1,0:T(8,128)S(1)} %get-tuple-element.354), custom_call_target="InvertDiagBlocksLowerTriangular" | custom-call | tf_op jit(solution)/shard_map/triangular_solve | solution.py:17
  (252 shorter events, 306.0 us)
Async XLA Ops:
  7.2 461.8 %all-reduce.6.cloned.1.call-start = ((), (), s32[]{:S(2)}) async-start(), calls=%async_computation | async-start | bytes 8388608 | tf_op jit(solution)/shard_map/psum | solution.py:108
  15.4 6.9 %copy-start.2 = (bf16[1,8,512,256]{2,3,1,0:T(8,128)(2,1)}, bf16[1,8,512,256]{2,3,1,0:T(8,128)(2,1)S(1)}, u32[]{:S(2)}) copy-start(bf16[1,8,512,256]{2,3,1,0:T(8,128)(2,1)S(1)} %copy.17) | copy-start | bytes 6291460
  15.9 2.1 copy-start
  18.0 4.2 copy-start.4
  168.3 28.0 %collective-permute-start = (f32[512,512]{0,1:T(8,128)S(1)}, f32[512,512]{0,1:T(8,128)S(1)}, u32[]{:S(2)}, u32[]{:S(2)}) collective-permute-start(f32[512,512]{0,1:T(8,128)S(1)} %slice_bitcast_fusion.1), channel_id=1, source_target_pairs={{1,0},{2,1},{3,2},{4,3},{5,4},{6,5},{7,6},{9,8},{10,9},{11,10},{12... | collective-permute-start | bytes 3145736 | tf_op jit(solution)/shard_map/ppermute | solution.py:13
  197.1 9.1 %copy-start.6 = (f32[1,4]{1,0:T(1,128)S(1)}, f32[1,4]{1,0:T(1,128)}, u32[]{:S(2)}) copy-start(f32[1,4]{1,0:T(1,128)} %param.23) | copy-start | bytes 52
  200.0 26.4 %collective-permute-start.1 = (f32[512,512]{0,1:T(8,128)}, f32[512,512]{0,1:T(8,128)}, u32[]{:S(2)}, u32[]{:S(2)}) collective-permute-start(f32[512,512]{0,1:T(8,128)} %convolution_bitcast_fusion.4), channel_id=1, source_target_pairs={{0,1},{1,2},{2,3},{3,4},{4,5},{5,6},{6,7},{8,9},{9,10},{10,11},{11... | collective-permute-start | bytes 3145736 | tf_op jit(solution)/shard_map/ppermute | solution.py:13
  206.1 20.3 %copy-start.1 = (f32[8,512,256]{1,2,0:T(8,128)S(1)}, f32[8,512,256]{1,2,0:T(8,128)}, u32[]{:S(2)}) copy-start(f32[8,512,256]{1,2,0:T(8,128)} %copy-done) | copy-start | bytes 12582916
  382.0 90.2 %copy-start.3 = (bf16[1,8,512,256]{2,3,1,0:T(8,128)(2,1)S(1)}, bf16[1,8,512,256]{2,3,1,0:T(8,128)(2,1)}, u32[]{:S(2)}) copy-start(bf16[1,8,512,256]{2,3,1,0:T(8,128)(2,1)} %copy-done.2) | copy-start | bytes 6291460
  382.0 228.9 %all-reduce.8.cloned.1.call-start = ((), (), s32[]{:S(2)}) async-start(), calls=%async_computation.1 | async-start | bytes 1048576 | tf_op jit(solution)/shard_map/psum | solution.py:115
  469.0 3.2 copy-start.5
Sparse Core Ops, SparseCore 0:
  382.1 86.7 all-reduce.5
  481.4 129.4 all-reduce.7
where the time goes:
time: 699 us; the launch traced here: 687 us
  waiting for transfers between devices  252 us (36%)
  other arithmetic  173 us (25%)
  local copies, waits for them, and re-layouts  128 us (18%)
  matrix products  104 us (15%)
  between operations  20.8 us (3%)
  starting transfers between devices  7.59 us (1%)
    psum x1, waiting for transfers between devices, on_device(): lax.psum((gram_part, projected_part), ('pole', 'dom'))  129 us
    dot_general x35, matrix products, complex_product(): jnp.dot(stacked, vectors.astype(jnp.bfloat16), preferred_element_type=jnp...  83.1 us
    dynamic_slice x64, local copies, waits for them, and re-layouts, partition_solve(): lax.scan(forward_step, initial, (inverse, source, previous))  82.9 us
    psum x1, waiting for transfers between devices, on_device(): summed = lax.psum(filtered_term, 'pole')  81.9 us
    dynamic_update_slice x32, other arithmetic, partition_solve(): lax.scan(forward_step, initial, (inverse, source, previous))  60.9 us
    ppermute x2, waiting for transfers between devices, shifted(): return lax.ppermute(x, axis, pairs)  41.1 us
    add x16, other arithmetic, backward_step(): partial_value + complex_product(block_inverse, real_product(couple_next,...  35.2 us
    another operation x7, other arithmetic, on_device(): factor = jnp.linalg.cholesky(gram)  34.8 us
  transfers between devices with their start and end apart: 4, of which 4 were waited for; matrix products, arithmetic and copies ran while one was open for 1% of the time, Pallas kernels for 0%

commit v1 on v0

--- a/solution.py
+++ b/solution.py
@@ -105,7 +105,9 @@
         - real_w * real_start
     )
     count = blocks // lax.axis_size("pole")
-    summed = lax.psum(filtered_term, "pole")
+    summed = filtered_term
+    for hop in (1, 2):
+        summed = summed + lax.ppermute(summed, "pole", [(dev, dev ^ hop) for dev in range(4)])
     offset = lax.axis_index("pole") * count
     own_rows = lax.dynamic_slice_in_dim(summed, offset, count, 0).reshape(count * B, M)
     gram_part = inner_products(own_rows, own_rows)

time: 699 us -> 721 us (1.031)
  waiting for transfers between devices: 252 us -> 265 us
  other arithmetic: 173 us -> 182 us
    ppermute x0 -> x2, waiting for transfers between devices: none -> 93.8 us  [on_device(): lax.ppermute(summed, 'pole', [(dev, dev ^ hop) for dev in range(4)])]
    psum x1 -> x0, waiting for transfers between devices: 81.9 us -> none  [on_device(): summed = lax.psum(filtered_term, 'pole')]
    add x0 -> x2, other arithmetic: none -> 9.29 us  [on_device(): summed + lax.ppermute(summed, 'pole', [(dev, dev ^ hop) for dev in range(...]
  transfers between devices with their start and end apart: 4 -> 5, of which waited for: 4 -> 5; matrix products, arithmetic and copies ran while one was open for 1% -> 1% of each run, Pallas kernels for 0% -> 0%
where the time goes in v1:
time: 721 us; the launch traced here: 709 us
  waiting for transfers between devices  265 us (37%)
  other arithmetic  182 us (25%)
  local copies, waits for them, and re-layouts  127 us (18%)
  matrix products  104 us (14%)
  between operations  21 us (3%)
  starting transfers between devices  9.01 us (1%)
    psum x1, waiting for transfers between devices, on_device(): lax.psum((gram_part, projected_part), ('pole', 'dom'))  130 us
    ppermute x2, waiting for transfers between devices, on_device(): lax.ppermute(summed, 'pole', [(dev, dev ^ hop) for dev in range(4)])  93.8 us
    dot_general x35, matrix products, complex_product(): jnp.dot(stacked, vectors.astype(jnp.bfloat16), preferred_element_type=jnp...  83.1 us
    dynamic_slice x64, local copies, waits for them, and re-layouts, partition_solve(): lax.scan(forward_step, initial, (inverse, source, previous))  82.9 us
    dynamic_update_slice x32, other arithmetic, partition_solve(): lax.scan(forward_step, initial, (inverse, source, previous))  60.9 us
    ppermute x2, waiting for transfers between devices, shifted(): return lax.ppermute(x, axis, pairs)  41.1 us
    add x16, other arithmetic, backward_step(): partial_value + complex_product(block_inverse, real_product(couple_next,...  35.4 us
    another operation x7, other arithmetic, on_device(): factor = jnp.linalg.cholesky(gram)  34.8 us
  transfers between devices with their start and end apart: 5, of which 5 were waited for; matrix products, arithmetic and copies ran while one was open for 1% of the time, Pallas kernels for 0%

profile of v1, /device:TPU:0, one launch (start us, length us, event | category | flops | bytes accessed | tf_op | source)
XLA Modules:
  0.0 709.0 jit_solution(16176408510340880278)
XLA Ops:
  7.2 4.2 slice_bitcast_fusion
  18.0 4.2 concatenate.76
  24.6 4.3 broadcast.158.clone.2
  29.8 65.2 %while.65 = (s32[]{:T(128)}, bf16[512,512]{0,1:T(8,128)(2,1)}, f32[8,512,512]{1,2,0:T(8,128)}, bf16[8,2,512,512]{3,2,1,0:T(8,128)(2,1)}, f32[8,512,512]{1,2,0:T(8,128)}, /*index=5*/bf16[8,512,512]{2,1,0:T(8,128)(2,1)}, s32[]{:T(128)}) while((s32[]{:T(128)}, bf16[512,512]{0,1:T(8,128)(2,1)}, f32[8,512,512]{1,2,0:T(8,128)}, ...), condition=%wide.region_1.2_spmd, body=%wide.region_0.1_spmd.sunk | while | flops 806617088 | bytes 17302612 | solution.py:62
  95.0 4.3 broadcast.158.clone.1
  99.3 67.8 %while.68 = (s32[]{:T(128)}, bf16[512,512]{0,1:T(8,128)(2,1)}, f32[8,512,512]{1,2,0:T(8,128)}, f32[8,512,512]{1,2,0:T(8,128)}, bf16[8,2,512,512]{3,2,1,0:T(8,128...) while((s32[]{:T(128)}, bf16[512,512]{0,1:T(8,128)(2,1)}, ...), condition=%wide.region_3.4_spmd.clone, body=%wide.region_2.3_spmd.clone.sunk | while | flops 807403520 | bytes 15204483 | solution.py:69
  174.0 22.5 %collective-permute-done = f32[512,512]{0,1:T(8,128)S(1)} collective-permute-done((f32[512,512]{0,1:T(8,128)S(1)}, f32[512,512]{0,1:T(8,128)S(1)}, u32[]{:S(2)}, u32[]{:S(2)}) %collective-permute-start) | collective-permute-done | bytes 1048608 | tf_op jit(solution)/shard_map/ppermute | solution.py:13
  200.2 6.1 collective-permute-start.1
  207.9 18.7 %collective-permute-done.1 = f32[512,512]{0,1:T(8,128)} collective-permute-done((f32[512,512]{0,1:T(8,128)}, f32[512,512]{0,1:T(8,128)}, u32[]{:S(2)}, u32[]{:S(2)}) %collective-permute-start.1) | collective-permute-done | bytes 1048608 | tf_op jit(solution)/shard_map/ppermute | solution.py:13
  231.8 4.3 broadcast.158.clone
  237.0 65.5 %while.66 = (s32[]{:T(128)}, bf16[512,512]{0,1:T(8,128)(2,1)}, f32[8,512,512]{1,2,0:T(8,128)}, bf16[8,2,512,512]{3,2,1,0:T(8,128)(2,1)}, f32[8,512,512]{1,2,0:T(8,128)}, /*index=5*/bf16[8,512,512]{2,1,0:T(8,128)(2,1)}, s32[]{:T(128)}) while((s32[]{:T(128)}, bf16[512,512]{0,1:T(8,128)(2,1)}, f32[8,512,512]{1,2,0:T(8,128)}, ...), condition=%wide.region_5.6_spmd, body=%wide.region_4.5_spmd.sunk | while | flops 806617088 | bytes 17302612 | solution.py:62
  302.5 4.3 broadcast.158
  306.9 67.9 %while.69 = (s32[]{:T(128)}, bf16[512,512]{0,1:T(8,128)(2,1)}, f32[8,512,512]{1,2,0:T(8,128)}, f32[8,512,512]{1,2,0:T(8,128)}, bf16[8,2,512,512]{3,2,1,0:T(8,128...) while((s32[]{:T(128)}, bf16[512,512]{0,1:T(8,128)(2,1)}, ...), condition=%wide.region_7.8_spmd.clone, body=%wide.region_6.7_spmd.clone.sunk | while | flops 807403520 | bytes 15204483 | solution.py:69
  374.8 6.3 multiply_subtract_fusion
  381.1 7.1 %collective-permute-done.2 = f32[8,512,256]{1,2,0:T(8,128)S(1)} collective-permute-done((f32[8,512,256]{1,2,0:T(8,128)S(1)}, f32[8,512,256]{1,2,0:T(8,128)S(1)}, u32[]{:S(2)}, u32[]{:S(2)}) %collective-permute-start.2) | collective-permute-done | bytes 4194336 | tf_op jit(solution)/shard_map/ppermute | solution.py:110
  388.3 4.8 fusion.125
  399.4 86.6 %collective-permute-done.3 = f32[8,512,256]{1,2,0:T(8,128)} collective-permute-done((f32[8,512,256]{1,2,0:T(8,128)}, f32[8,512,256]{1,2,0:T(8,128)}, u32[]{:S(2)}, u32[]{:S(2)}) %collective-permute-start.3) | collective-permute-done | bytes 4194336 | tf_op jit(solution)/shard_map/ppermute | solution.py:110
  486.0 4.5 add.174
  492.3 9.1 %fusion.61 = f32[256,256]{0,1:T(8,128)} fusion(f32[8,512,256]{1,2,0:T(8,128)S(1)} %add.174, f32[8,512,512]{1,2,0:T(8,128)} %get-tuple-element.338, f32[]{:T(128)S(6)} %add.177, f32[]{:T(128)S(6)} %sub.71, f32[]{:T(128)} %bitcast.8, bf16[1,8,512,256]{2,3,1,0:T(8,128)(2,1)S(1)} %copy-done.4), kind=kOutput, calls=%fused_computation.81 | convolution fusion | flops 3227516928 | bytes 14942220 | tf_op jit(solution)/shard_map/dot_general | solution.py:44
  501.8 130.4 %all-reduce.5.cloned.1.call-done = (f32[256,256]{0,1:T(8,128)}, f32[256,256]{0,1:T(8,128)}) async-done(((f32[256,256]{0,1:T(8,128)}, f32[256,256]{0,1:T(8,128)}), (f32[256,256]{0,1:T(8,128)}, f32[256,256]{0,1:T(8,128)})) %all-reduce.5.cloned.1.call-update) | async-done | bytes 524304 | tf_op jit(solution)/shard_map/psum | solution.py:117
  634.4 11.9 %cholesky.50 = f32[128,128]{1,0:T(8,128)S(1)} custom-call(f32[128,128]{1,0:T(8,128)S(1)} %cholesky.118), custom_call_target="Cholesky" | custom-call | tf_op jit(solution)/shard_map/jit(cholesky)/cholesky | solution.py:121
  646.4 9.8 %custom-call.17 = f32[1,128,128]{1,2,0:T(8,128)S(1)} custom-call(f32[1,128,128]{2,1,0:T(8,128)S(1)} %get-tuple-element.517), custom_call_target="InvertDiagBlocksLowerTriangular" | custom-call | tf_op jit(solution)/shard_map/jit(cholesky)/cholesky | solution.py:121
  656.7 11.7 %cholesky.105 = f32[128,128]{1,0:T(8,128)S(1)} custom-call(f32[128,128]{1,0:T(8,128)S(1)} %convolution_subtract_fusion.1), custom_call_target="Cholesky" | custom-call | tf_op jit(solution)/shard_map/jit(cholesky)/cholesky | solution.py:121
  675.1 19.9 %custom-call.18 = f32[2,128,128]{1,2,0:T(8,128)S(1)} custom-call(f32[2,128,128]{2,1,0:T(8,128)S(1)} %get-tuple-element.354), custom_call_target="InvertDiagBlocksLowerTriangular" | custom-call | tf_op jit(solution)/shard_map/triangular_solve | solution.py:17
  (255 shorter events, 316.0 us)
Async XLA Ops:
  7.2 625.1 %all-reduce.5.cloned.1.call-start = ((), (), s32[]{:S(2)}) async-start(), calls=%async_computation | async-start | bytes 1048576 | tf_op jit(solution)/shard_map/psum | solution.py:117
  15.4 6.9 copy-start.3
  16.0 2.1 copy-start.1
  18.0 4.3 copy-start.5
  168.4 28.0 %collective-permute-start = (f32[512,512]{0,1:T(8,128)S(1)}, f32[512,512]{0,1:T(8,128)S(1)}, u32[]{:S(2)}, u32[]{:S(2)}) collective-permute-start(f32[512,512]{0,1:T(8,128)S(1)} %slice_bitcast_fusion.1), channel_id=1, source_target_pairs={{1,0},{2,1},{3,2},{4,3},{5,4},{6,5},{7,6},{9,8},{10,9},{11,10},{12... | collective-permute-start | bytes 3145736 | tf_op jit(solution)/shard_map/ppermute | solution.py:13
  197.2 9.1 %copy-start.6 = (f32[1,4]{1,0:T(1,128)S(1)}, f32[1,4]{1,0:T(1,128)}, u32[]{:S(2)}) copy-start(f32[1,4]{1,0:T(1,128)} %param.23) | copy-start | bytes 52
  200.2 26.4 %collective-permute-start.1 = (f32[512,512]{0,1:T(8,128)}, f32[512,512]{0,1:T(8,128)}, u32[]{:S(2)}, u32[]{:S(2)}) collective-permute-start(f32[512,512]{0,1:T(8,128)} %convolution_bitcast_fusion.4), channel_id=1, source_target_pairs={{0,1},{1,2},{2,3},{3,4},{4,5},{5,6},{6,7},{8,9},{9,10},{10,11},{11... | collective-permute-start | bytes 3145736 | tf_op jit(solution)/shard_map/ppermute | solution.py:13
  206.3 20.3 %copy-start.2 = (f32[8,512,256]{1,2,0:T(8,128)S(1)}, f32[8,512,256]{1,2,0:T(8,128)}, u32[]{:S(2)}) copy-start(f32[8,512,256]{1,2,0:T(8,128)} %copy-done.1) | copy-start | bytes 12582916
  374.7 13.5 %copy-start = (f32[8,512,512]{1,2,0:T(8,128)S(1)}, f32[8,512,512]{1,2,0:T(8,128)}, u32[]{:S(2)}) copy-start(f32[8,512,512]{1,2,0:T(8,128)} %get-tuple-element.338) | copy-start | bytes 25165828
  381.0 7.2 %collective-permute-start.2 = (f32[8,512,256]{1,2,0:T(8,128)S(1)}, f32[8,512,256]{1,2,0:T(8,128)S(1)}, u32[]{:S(2)}, u32[]{:S(2)}) collective-permute-start(f32[8,512,256]{1,2,0:T(8,128)S(1)} %multiply_subtract_fusion), channel_id=1, source_target_pairs={{0,8},{8,0},{16,24},{24,16},{1,9},{9,1},{17,25},{25,17},{2,10},{10... | collective-permute-start | bytes 12582920 | tf_op jit(solution)/shard_map/ppermute | solution.py:110
  393.1 92.9 %collective-permute-start.3 = (f32[8,512,256]{1,2,0:T(8,128)}, f32[8,512,256]{1,2,0:T(8,128)}, u32[]{:S(2)}, u32[]{:S(2)}) collective-permute-start(f32[8,512,256]{1,2,0:T(8,128)} %fusion.125), channel_id=1, source_target_pairs={{0,16},{8,24},{16,0},{24,8},{1,17},{9,25},{17,1},{25,9},{2,18},{10... | collective-permute-start | bytes 12582920 | tf_op jit(solution)/shard_map/ppermute | solution.py:110
  490.5 1.8 copy-start.4
Sparse Core Ops, SparseCore 0:
  501.5 130.6 all-reduce.4
